TPU v7x, 128 devices: a whole 4x4x4 slice. The times are simulated.
128 devices in a mesh: rows: 16 (over z, x), cols: 8 (over y, core).
Axes of the slice: x: 4, y: 4, z: 4, core: 2. Of those that a mesh axis runs over, the one named last changes fastest.
Arguments:
- densities: bfloat16 [6, 8192, 128, 128], P(None, ('rows', 'cols')), may hold values from -6 to 6
- residuals: bfloat16 [6, 8192, 128, 128], P(None, ('rows', 'cols')), may hold values from -32 to 32
- block_pairs: int32 [2, 8192], P(None, ('rows', 'cols')), may hold values from 0 to 1562
- new_owner: int32 [8192], P(('rows', 'cols')), may hold values from -1 to 15, as said below
Outputs:
- owned_blocks: bfloat16 [4096, 128, 128], P(('rows', 'cols'))
- coefficients: float32 [6], replicated
Inputs may be any that keep to these rules, and one draw needn't show every extreme that they name: A live block stays at its index of cols and moves to index new_owner of rows. For each index of cols, every index of rows becomes the owner of exactly 32 blocks, and at most 4 of them come from one device.
All inputs are finite; a program needn't handle non-finite values.
Results may differ from a plain program's by a relative error of at most 0.0019.
Values may be sent and summed in bfloat16 or wider, within the bound.
A program may use at most 128 MiB of HBM per device.

v0:
```python
import math

import jax
import jax.numpy as jnp
from jax import lax
from jax.sharding import Mesh
from jax.sharding import PartitionSpec as P

OWNED = 32
ROWS = ("rows_0", "rows_1")
ROWS_COLS = ("rows_0", "rows_1", "cols_0", "cols_1")


mix_weight = 0.3


def over_axes(shard, axes):
    for axis in axes:
        shard = lax.psum(shard, axis)
    return shard


def sent_together(arrays, axis, split_dim, concat_dim, along):
    widths = [math.prod(a.shape[along:]) for a in arrays]
    both = jnp.concatenate(
        [a.reshape(*a.shape[:along], w) for a, w in zip(arrays, widths)], axis=along
    )
    whole = lax.all_to_all(both, axis, split_axis=split_dim, concat_axis=concat_dim, tiled=True)
    pieces = jnp.split(whole, [sum(widths[:k]) for k in range(1, len(widths))], axis=along)
    return tuple(
        (b.reshape(*whole.shape[:along], *a.shape[along:]) for a, b in zip(arrays, pieces))
    )


def small_solve(system, vector):
    order_n = system.shape[0]
    positions = jnp.arange(order_n, dtype=jnp.int32)
    for step_index in range(order_n):
        column = system[:, step_index] / system[step_index, step_index]
        column = jnp.where(positions > step_index, column, 0.0)
        system = system - column[:, None] * system[step_index][None, :]
        vector = vector - column * vector[step_index]
    solution = jnp.zeros((order_n,), jnp.float32)
    for step_index in reversed(range(order_n)):
        inner = jnp.sum(jnp.where(positions > step_index, system[step_index] * solution, 0.0))
        solution = solution.at[step_index].set(
            (vector[step_index] - inner) / system[step_index, step_index]
        )
    return solution


def slot_correlation(residual_set, weights):
    flattened = residual_set.reshape(residual_set.shape[0], residual_set.shape[1], -1)
    per_slot = jnp.einsum("isn,ksn->sik", flattened, flattened, preferred_element_type=jnp.float32)
    return jnp.einsum("s,sik->ik", weights, per_slot)


def blend_history(density_set, residual_set, coefficients):
    running = jnp.zeros(density_set.shape[1:], jnp.float32)
    for hist_index in range(density_set.shape[0]):
        running = running + coefficients[hist_index] * (
            density_set[hist_index].astype(jnp.float32)
            + mix_weight * residual_set[hist_index].astype(jnp.float32)
        )
    return running.astype(jnp.bfloat16)


def compact_order(arrived_weights):
    usable = arrived_weights > 0.0
    position = jnp.cumsum(usable.astype(jnp.int32)) - 1
    spots = jnp.where(usable, position, OWNED)
    count_in = arrived_weights.shape[0]
    return (
        jnp.zeros((OWNED,), jnp.int32)
        .at[spots]
        .set(jnp.arange(count_in, dtype=jnp.int32), mode="drop")
    )


def on_device(densities, residuals, block_pairs, new_owner):
    rows_count = lax.axis_size(ROWS)
    held_slots = new_owner.shape[0]
    pair_cap = 2 * OWNED // rows_count
    sent_count = rows_count * pair_cap
    alive_slot = new_owner >= 0
    weights = jnp.where(
        alive_slot, jnp.where(block_pairs[0] == block_pairs[1], 1.0, 2.0), 0.0
    ).astype(jnp.float32)
    owner_rows = jnp.where(alive_slot, new_owner, rows_count)
    onehot = (owner_rows[:, None] == jnp.arange(rows_count, dtype=jnp.int32)[None, :]).astype(
        jnp.int32
    )
    ranking = jnp.sum(jnp.cumsum(onehot, axis=0) * onehot, axis=1) - 1
    placing = jnp.where(alive_slot, owner_rows * pair_cap + ranking, sent_count)
    slot_table = (
        jnp.full((sent_count,), held_slots, jnp.int32)
        .at[placing]
        .set(jnp.arange(held_slots, dtype=jnp.int32), mode="drop")
    )
    chosen = jnp.minimum(slot_table, held_slots - 1)
    sent_weights = jnp.where(slot_table < held_slots, weights[chosen], 0.0).astype(jnp.bfloat16)
    partial_correlation = slot_correlation(residuals, weights)
    correlation = over_axes(partial_correlation, ROWS_COLS)
    solved = small_solve(correlation, jnp.ones((correlation.shape[0],), jnp.float32))
    coefficients = solved / jnp.sum(solved)
    mixed_blocks = blend_history(densities, residuals, coefficients)
    arrived = sent_together((jnp.take(mixed_blocks, chosen, axis=0), sent_weights), ROWS, 0, 0, 1)
    ordering = compact_order(arrived[1].astype(jnp.float32))
    owned_blocks = jnp.take(arrived[0], ordering, axis=0)
    return (owned_blocks, coefficients)


def solution(mesh):
    finer = Mesh(mesh.devices.reshape(4, 4, 4, 2), ("rows_0", "rows_1", "cols_0", "cols_1"))
    placed = (
        P(None, ROWS_COLS, None, None),
        P(None, ROWS_COLS, None, None),
        P(None, ROWS_COLS),
        P(ROWS_COLS),
    )
    return jax.shard_map(
        on_device,
        mesh=finer,
        in_specs=placed,
        out_specs=(P(ROWS_COLS, None, None), P()),
        check_vma=False,
    )
```

profile of v0, /device:TPU:1, one launch (start us, length us, event | category | flops | bytes accessed | tf_op | source)
XLA Modules:
  0.0 181.8 jit_solution(14039004211042699980)
XLA Ops:
  0.6 19.3 %reshape.282 = bf16[6,64,16384]{2,1,0:T(8,128)(2,1)} reshape(bf16[6,64,128,128]{3,2,1,0:T(8,128)(2,1)} %param.17) | data formatting | bytes 25165824 | tf_op jit(solution)/shard_map/reshape | solution.py:53
  20.0 25.8 %fusion = bf16[64,6,6]{2,1,0:T(8,128)(2,1)S(1)} fusion(bf16[6,64,16384]{2,1,0:T(8,128)(2,1)} %reshape.282), kind=kOutput, calls=%fused_computation.5 | convolution fusion | flops 75497472 | bytes 12587520 | tf_op jit(solution)/shard_map/isn,ksn->sik/dot_general | solution.py:54
  45.9 10.5 %psum.28 = f32[6,6]{1,0:T(8,128)S(1)} all-reduce(f32[6,6]{1,0:T(8,128)S(1)} %bitcast.87), channel_id=1, replica_groups=mesh['rows_0'=4,'rows_1'=4,'cols_0'=4,'cols_1'=2] {'rows_0'}, use_global_device_ids=true, to_apply=%region_3.4 | all-reduce | flops 36 | bytes 288 | tf_op jit(solution)/shard_map/psum | solution.py:19
  56.5 8.8 %psum.29 = f32[6,6]{1,0:T(8,128)S(1)} all-reduce(f32[6,6]{1,0:T(8,128)S(1)} %psum.28), channel_id=1, replica_groups=mesh['rows_0'=4,'rows_1'=4,'cols_0'=4,'cols_1'=2] {'rows_1'}, use_global_device_ids=true, to_apply=%region_4.5 | all-reduce | flops 36 | bytes 288 | tf_op jit(solution)/shard_map/psum | solution.py:19
  65.2 8.7 %psum.30 = f32[6,6]{1,0:T(8,128)S(1)} all-reduce(f32[6,6]{1,0:T(8,128)S(1)} %psum.29), channel_id=1, replica_groups=mesh['rows_0'=4,'rows_1'=4,'cols_0'=4,'cols_1'=2] {'cols_0'}, use_global_device_ids=true, to_apply=%region_5.6 | all-reduce | flops 36 | bytes 288 | tf_op jit(solution)/shard_map/psum | solution.py:19
  73.9 8.6 %psum.31 = f32[6,6]{1,0:T(8,128)S(1)} all-reduce(f32[6,6]{1,0:T(8,128)S(1)} %psum.30), channel_id=1, replica_groups=mesh['rows_0'=4,'rows_1'=4,'cols_0'=4,'cols_1'=2] {'cols_1'}, use_global_device_ids=true, to_apply=%region_6.7 | all-reduce | flops 36 | bytes 288 | tf_op jit(solution)/shard_map/psum | solution.py:19
  83.0 0.8 fusion.7
  84.5 0.8 select_reduce_fusion.5
  86.0 0.8 select_reduce_fusion.4
  87.5 0.8 select_reduce_fusion.3
  89.0 0.8 select_reduce_fusion.2
  90.5 0.8 select_reduce_fusion.1
  117.0 1.0 scatter_custom_fusion
  118.7 15.0 %fusion.2 = bf16[64,128,128]{2,1,0:T(8,128)(2,1)S(1)} fusion(bf16[6,64,128,128]{3,2,1,0:T(8,128)(2,1)} %param.17, bf16[6,64,128,128]{3,2,1,0:T(8,128)(2,1)} %param.16, f32[]{:T(128)} %bitcast.49, f32[]{:T(128)} %bitcast.48, f32[]{:T(128)} %bitcast.47, f32[]{:T(128)} %bitcast.46, f32[]{:T(128)} %bitcast.45, f32[]{:T(128)} %bitcast.44), kind=kLoop, calls=%fused_computation.11 | loop fusion | flops 37748736 | bytes 27263000 | tf_op jit(solution)/shard_map/convert_element_type | solution.py:65
  133.7 2.2 %gather_fusion = bf16[64,128,128]{2,1,0:T(8,128)(2,1)} fusion(bf16[64,128,128]{2,1,0:T(8,128)(2,1)S(1)} %fusion.2, s32[1024]{0:T(1024)S(1)} %pad_clamp_fusion.1), kind=kCustom, calls=%fused_computation | custom fusion | bytes 4194560 | tf_op jit(solution)/shard_map/jit(_take)/gather | solution.py:107
  135.9 2.6 %gather.14 = bf16[16,4,16384]{2,1,0:T(4,128)(2,1)S(1)} reshape(bf16[64,128,128]{2,1,0:T(8,128)(2,1)} %gather_fusion) | data formatting | bytes 4194304 | tf_op jit(solution)/shard_map/jit(_take)/gather | solution.py:107
  138.8 1.0 broadcast_select_fusion
  139.8 1.0 pad_maximum_fusion
  140.8 31.6 %all_to_all.9 = bf16[16,4,16385]{2,1,0:T(4,128)(2,1)} all-to-all(bf16[16,4,16385]{2,1,0:T(4,128)(2,1)S(1)} %pad_maximum_fusion), channel_id=1, replica_groups=mesh['rows_0'=4,'rows_1'=4,'cols_0'=4,'cols_1'=2] {'rows_0','rows_1'}, dimensions={0} | all-to-all | bytes 4194560 | tf_op jit(solution)/shard_map/all_to_all | solution.py:28
  172.3 2.8 %all_to_all.7 = bf16[64,16385]{1,0:T(8,128)(2,1)S(1)} reshape(bf16[16,4,16385]{2,1,0:T(4,128)(2,1)} %all_to_all.9) | data formatting | bytes 4194560 | tf_op jit(solution)/shard_map/all_to_all | solution.py:28
  175.2 1.5 slice_bitcast_fusion
  176.9 0.8 scatter_custom_fusion.1
  177.7 2.2 %copy.11 = bf16[8,8,128,128]{3,2,1,0:T(8,128)(2,1)S(1)} copy(bf16[8,8,128,128]{3,1,2,0:T(8,128)(2,1)} %slice_bitcast_fusion) | data formatting | bytes 4194304
  180.7 1.1 broadcast_select_fusion.1
  (75 shorter events, 20.0 us)
Async XLA Ops:
  20.0 25.8 %copy-start.1 = (s32[2,64]{1,0:T(2,128)S(1)}, s32[2,64]{1,0:T(2,128)}, u32[]{:S(2)}) copy-start(s32[2,64]{1,0:T(2,128)} %param.18) | copy-start | bytes 1540
  20.0 25.8 %copy-start.2 = (s32[64]{0:T(128)S(1)}, s32[64]{0:T(128)}, u32[]{:S(2)}) copy-start(s32[64]{0:T(128)} %param.19) | copy-start | bytes 772
  115.9 17.8 %copy-start = (f32[6]{0:T(128)}, f32[6]{0:T(128)S(1)}, u32[]{:S(2)}) copy-start(f32[6]{0:T(128)S(1)} %broadcast_divide_fusion) | copy-start | bytes 76
where the time goes:
time: 183 us; the launch traced here: 182 us
  blocking collectives  68.2 us (37%)
  local copies, waits for them, and re-layouts  42.7 us (23%)
  other arithmetic  32.5 us (18%)
  matrix products  25.9 us (14%)
  between operations  12.5 us (7%)
    psum x4, blocking collectives, over_axes(): shard = lax.psum(shard, axis)  36.6 us
    all_to_all x1, blocking collectives, sent_together(): lax.all_to_all(both, axis, split_axis=split_dim, concat_axis=concat_dim,...  31.6 us
    dot_general x1, matrix products, slot_correlation(): jnp.einsum('isn,ksn->sik', flattened, flattened, preferred_element_type=j...  25.8 us
    reshape x1, local copies, waits for them, and re-layouts, slot_correlation(): residual_set.reshape(residual_set.shape[0], residual_set.shape[1], -1)  19.3 us
    convert_element_type x1, other arithmetic, blend_history(): return running.astype(jnp.bfloat16)  15 us
    gather x2, local copies, waits for them, and re-layouts, on_device(): jnp.take(mixed_blocks, chosen, axis=0)  4.79 us
    select_n x5, other arithmetic, small_solve(): column = jnp.where(positions > step_index, column, 0.0)  4.13 us
    reduce_sum x6, other arithmetic, small_solve(): jnp.sum(jnp.where(positions > step_index, system[step_index] * solution,...  3.92 us

commit v1 on v0

v1 whole, which is shorter than its diff:
```python
import functools

import jax
import jax.numpy as jnp
from jax import lax
from jax.experimental import pallas as pl
from jax.experimental.pallas import tpu as pltpu
from jax.sharding import PartitionSpec as P

MESH = pl.DeviceIdType.MESH

HIST = 6
HELD = 64
OWNED = 32
BLOCK = 128
CAP = 4
CHUNK = 4
N_CHUNKS = HELD // CHUNK
GROUP = 32
STACK = HIST * GROUP

mix_weight = 0.3


def kernel(
    n_rows,
    n_cols,
    dens_hbm,
    res_hbm,
    pairs,
    owner,
    owner_row,
    owned,
    coef_out,
    dens,
    res,
    acc,
    outgoing,
    arrived,
    cols_in,
    rows_in,
    cols_out,
    rows_out,
    counts_in,
    counts_out,
    table_v,
    table_s,
    order_v,
    order_s,
    res_sem,
    dens_sem,
    cols_send,
    cols_recv,
    rows_send,
    rows_recv,
    counts_send,
    counts_recv,
    move_send,
    move_recv,
    table_sem,
):
    my_row = lax.axis_index("rows")
    my_col = lax.axis_index("cols")

    def chunk_copy(src, dst, sem, c):
        part = pl.ds(c * CHUNK, CHUNK)
        return pltpu.make_async_copy(src.at[:, part], dst.at[:, part], sem.at[c])

    for c in range(N_CHUNKS):
        chunk_copy(res_hbm, res, res_sem, c).start()

    row_peers = [lax.rem(my_row + o, n_rows) for o in range(1, n_rows)]
    col_peers = [lax.rem(my_col + o, n_cols) for o in range(1, n_cols)]

    barrier = pltpu.get_barrier_semaphore()
    for r in row_peers:
        pl.semaphore_signal(barrier, inc=1, device_id={"rows": r}, device_id_type=MESH)
    for c in col_peers:
        pl.semaphore_signal(barrier, inc=1, device_id={"cols": c}, device_id_type=MESH)

    own = jnp.broadcast_to(owner_row[...], (HELD, HELD))
    down = lax.broadcasted_iota(jnp.int32, (HELD, HELD), 0)
    across = lax.broadcasted_iota(jnp.int32, (HELD, HELD), 1)
    own_down = jnp.sum(jnp.where(down == across, own, 0), axis=1, keepdims=True)
    same_before = (own == own_down) & (across < down)
    rank_down = jnp.sum(jnp.where(same_before, 1, 0), axis=1, keepdims=True)
    place_down = jnp.where(own_down >= 0, own_down * CAP + rank_down, -1)
    table_v[...] = jnp.sum(jnp.where(place_down == across, down, 0), axis=0, keepdims=True)
    lanes = lax.broadcasted_iota(jnp.int32, (HELD, BLOCK), 1)
    counts_out[...] = jnp.sum(jnp.where(own_down == lanes, 1, 0), axis=0, keepdims=True)
    table_copy = pltpu.make_async_copy(table_v, table_s, table_sem.at[0])
    table_copy.start()

    acc[...] = jnp.zeros_like(acc)

    def gram_slot(s):
        live = owner[s] >= 0
        weight = jnp.where(live, jnp.where(pairs[0, s] == pairs[1, s], 1.0, 2.0), 0.0)
        parts = [
            res[:, s, pl.ds(g * GROUP, GROUP), :].reshape(STACK, BLOCK)
            for g in range(BLOCK // GROUP)
        ]
        left = jnp.concatenate(parts, axis=1)
        return left, left * weight.astype(jnp.bfloat16)

    def gram_chunk(c, carry):
        chunk_copy(res_hbm, res, res_sem, c).wait()
        chunk_copy(dens_hbm, dens, dens_sem, c).start()
        for h in range(CHUNK // 2):
            pieces = [gram_slot(c * CHUNK + h * 2 + j) for j in range(2)]
            left = jnp.concatenate([p[0] for p in pieces], axis=1)
            right = jnp.concatenate([p[1] for p in pieces], axis=1)
            acc[...] += lax.dot_general(
                left, right, (((1,), (1,)), ((), ())), preferred_element_type=jnp.float32
            )
        return carry

    lax.fori_loop(0, N_CHUNKS, gram_chunk, 0)

    x_down = lax.broadcasted_iota(jnp.int32, (STACK, STACK), 0)
    x_across = lax.broadcasted_iota(jnp.int32, (STACK, STACK), 1)
    same_x = lax.rem(x_down, GROUP) == lax.rem(x_across, GROUP)
    diag = jnp.where(same_x, acc[...], 0.0).reshape(HIST, GROUP, STACK)
    by_iterate = jnp.sum(diag, axis=1)
    seg = lax.broadcasted_iota(jnp.int32, (HIST, STACK), 1) // GROUP
    i_at = lax.broadcasted_iota(jnp.int32, (HIST, BLOCK), 0)
    lane_at = lax.broadcasted_iota(jnp.int32, (HIST, BLOCK), 1)
    packed = jnp.zeros((HIST, BLOCK), jnp.float32)
    for k in range(HIST):
        entry = jnp.sum(jnp.where(seg == k, by_iterate, 0.0), axis=1, keepdims=True)
        packed = jnp.where(lane_at == i_at * 8 + k, entry, packed)
    row = jnp.sum(packed, axis=0, keepdims=True)

    pl.semaphore_wait(barrier, n_rows + n_cols - 2)

    cols_out[...] = row
    cols_in[my_col] = row

    def cols_copy(peer, slot):
        return pltpu.make_async_remote_copy(
            src_ref=cols_out,
            dst_ref=cols_in.at[slot],
            send_sem=cols_send.at[peer],
            recv_sem=cols_recv.at[slot],
            device_id={"cols": peer},
            device_id_type=MESH,
        )

    def rows_copy(peer, slot):
        return pltpu.make_async_remote_copy(
            src_ref=rows_out,
            dst_ref=rows_in.at[slot],
            send_sem=rows_send.at[peer],
            recv_sem=rows_recv.at[slot],
            device_id={"rows": peer},
            device_id_type=MESH,
        )

    def counts_copy(peer, slot):
        return pltpu.make_async_remote_copy(
            src_ref=counts_out,
            dst_ref=counts_in.at[slot],
            send_sem=counts_send.at[peer],
            recv_sem=counts_recv.at[slot],
            device_id={"rows": peer},
            device_id_type=MESH,
        )

    def move_copy(peer, slot):
        return pltpu.make_async_remote_copy(
            src_ref=outgoing.at[peer],
            dst_ref=arrived.at[pl.ds(slot * CAP, CAP)],
            send_sem=move_send.at[peer],
            recv_sem=move_recv.at[slot],
            device_id={"rows": peer},
            device_id_type=MESH,
        )

    for c in col_peers:
        cols_copy(c, my_col).start()
    counts_in[my_row] = counts_out[...]
    for r in row_peers:
        counts_copy(r, my_row).start()
    for c in col_peers:
        cols_copy(c, c).wait_recv()
    row = jnp.sum(cols_in[...], axis=0)
    rows_out[...] = row
    rows_in[my_row] = row
    for r in row_peers:
        rows_copy(r, my_row).start()
    for c in range(N_CHUNKS):
        chunk_copy(dens_hbm, dens, dens_sem, c).wait()
    table_copy.wait()
    for r in row_peers:
        rows_copy(r, r).wait_recv()
    total = jnp.sum(rows_in[...], axis=0)

    def spread(i, k):
        return jnp.broadcast_to(total[:, i * 8 + k : i * 8 + k + 1], (8, BLOCK))

    a = {(i, k): spread(i, k) for i in range(HIST) for k in range(i, HIST)}
    b = [jnp.ones((8, BLOCK), jnp.float32) for _ in range(HIST)]
    for j in range(HIST):
        for i in range(j + 1, HIST):
            factor = a[j, i] / a[j, j]
            for k in range(i, HIST):
                a[i, k] = a[i, k] - factor * a[j, k]
            b[i] = b[i] - factor * b[j]
    solved = [None] * HIST
    for j in reversed(range(HIST)):
        inner = b[j]
        for k in range(j + 1, HIST):
            inner = inner - a[j, k] * solved[k]
        solved[j] = inner / a[j, j]
    norm = functools.reduce(lambda p, q: p + q, solved)
    coef = [s / norm for s in solved]
    lane = lax.broadcasted_iota(jnp.int32, (8, BLOCK), 1)
    shown = jnp.zeros((8, BLOCK), jnp.float32)
    for i in range(HIST):
        shown = jnp.where(lane == i, coef[i], shown)
    coef_out[...] = shown

    coef_d = [c[0:1, :] for c in coef]
    coef_r = [c[0:1, :] * mix_weight for c in coef]

    def blend(q, k):
        slot = table_s[0, q * CAP + k]
        running = None
        for i in range(HIST):
            term = coef_d[i] * dens[i, slot].astype(jnp.float32)
            running = term if running is None else running + term
            running = running + coef_r[i] * res[i, slot].astype(jnp.float32)
        return running.astype(jnp.bfloat16)

    def send_step(o, carry):
        q = lax.rem(my_row + o, n_rows)
        for k in range(CAP):
            outgoing[q, k] = blend(q, k)
        move_copy(q, my_row).start()
        return carry

    lax.fori_loop(1, n_rows, send_step, 0)
    for k in range(CAP):
        arrived[my_row * CAP + k] = blend(my_row, k)

    for r in row_peers:
        counts_copy(r, r).wait_recv()
    counts = counts_in[...].reshape(n_rows, BLOCK)
    lanes = lax.broadcasted_iota(jnp.int32, (n_rows, BLOCK), 1)
    count_down = jnp.sum(jnp.where(lanes == my_row, counts, 0), axis=1, keepdims=True)
    row_down = lax.broadcasted_iota(jnp.int32, (n_rows, BLOCK), 0)
    count_across = jnp.sum(
        jnp.where(lanes == row_down, count_down, 0), axis=0, keepdims=True
    )
    upto_down = jnp.sum(
        jnp.where(lanes <= row_down, count_across, 0), axis=1, keepdims=True
    )
    skipped = jnp.sum(
        jnp.where(upto_down <= lanes, CAP - count_down, 0), axis=0, keepdims=True
    )
    place = lax.broadcasted_iota(jnp.int32, (1, BLOCK), 1)
    order_v[...] = jnp.minimum(place + skipped, n_rows * CAP - 1)
    order_copy = pltpu.make_async_copy(order_v, order_s, table_sem.at[1])
    order_copy.start()
    order_copy.wait()

    for r in row_peers:
        move_copy(r, r).wait_recv()

    def keep(p, carry):
        owned[p] = arrived[order_s[0, p]]
        return carry

    lax.fori_loop(0, OWNED, keep, 0)

    for c in col_peers:
        cols_copy(c, my_col).wait_send()
    for r in row_peers:
        counts_copy(r, my_row).wait_send()
        rows_copy(r, my_row).wait_send()
        move_copy(r, my_row).wait_send()


def solution(mesh):
    n_rows, n_cols = mesh.shape["rows"], mesh.shape["cols"]

    def on_device(densities, residuals, block_pairs, new_owner):
        vmem = pltpu.VMEM
        dma = pltpu.SemaphoreType.DMA
        owned, coef = pl.pallas_call(
            functools.partial(kernel, n_rows, n_cols),
            out_shape=(
                jax.ShapeDtypeStruct((OWNED, BLOCK, BLOCK), jnp.bfloat16),
                jax.ShapeDtypeStruct((8, BLOCK), jnp.float32),
            ),
            in_specs=[
                pl.BlockSpec(memory_space=pl.ANY),
                pl.BlockSpec(memory_space=pl.ANY),
                pl.BlockSpec(memory_space=pltpu.SMEM),
                pl.BlockSpec(memory_space=pltpu.SMEM),
                pl.BlockSpec(memory_space=pltpu.VMEM),
            ],
            out_specs=(
                pl.BlockSpec(memory_space=pltpu.VMEM),
                pl.BlockSpec(memory_space=pltpu.VMEM),
            ),
            scratch_shapes=[
                vmem((HIST, HELD, BLOCK, BLOCK), jnp.bfloat16),
                vmem((HIST, HELD, BLOCK, BLOCK), jnp.bfloat16),
                vmem((STACK, STACK), jnp.float32),
                vmem((n_rows, CAP, BLOCK, BLOCK), jnp.bfloat16),
                vmem((n_rows * CAP, BLOCK, BLOCK), jnp.bfloat16),
                vmem((n_cols, 1, BLOCK), jnp.float32),
                vmem((n_rows, 1, BLOCK), jnp.float32),
                vmem((1, BLOCK), jnp.float32),
                vmem((1, BLOCK), jnp.float32),
                vmem((n_rows, 1, BLOCK), jnp.int32),
                vmem((1, BLOCK), jnp.int32),
                vmem((1, HELD), jnp.int32),
                pltpu.SMEM((1, HELD), jnp.int32),
                vmem((1, BLOCK), jnp.int32),
                pltpu.SMEM((1, BLOCK), jnp.int32),
                dma((N_CHUNKS,)),
                dma((N_CHUNKS,)),
                dma((n_cols,)),
                dma((n_cols,)),
                dma((n_rows,)),
                dma((n_rows,)),
                dma((n_rows,)),
                dma((n_rows,)),
                dma((n_rows,)),
                dma((n_rows,)),
                dma((2,)),
            ],
            compiler_params=pltpu.CompilerParams(
                collective_id=0, has_side_effects=True, vmem_limit_bytes=48 * 1024 * 1024
            ),
        )(densities, residuals, block_pairs, new_owner, new_owner.reshape(1, HELD))
        return owned, coef[0, :HIST]

    placed = P(None, ("rows", "cols"), None, None)
    return jax.shard_map(
        on_device,
        mesh=mesh,
        in_specs=(placed, placed, P(None, ("rows", "cols")), P(("rows", "cols"))),
        out_specs=(P(("rows", "cols"), None, None), P()),
        check_vma=False,
    )
```

time: 183 us -> 54.6 us (0.30)
  blocking collectives: 68.2 us -> 0 us
  Pallas kernels: 0 us -> 50.1 us
  local copies, waits for them, and re-layouts: 42.7 us -> 2.81 us
  other arithmetic: 32.5 us -> 0 us
  matrix products: 25.9 us -> 0 us
  between operations: 12.5 us -> 0.65 us
    pallas_call x0 -> x1, Pallas kernels: none -> 50.1 us  [on_device(): pl.pallas_call(functools.partial(kernel, n_rows, n_cols), out_shape=(jax....]
    psum x4 -> x0, blocking collectives: 36.6 us -> none  [over_axes(): shard = lax.psum(shard, axis)]
    all_to_all x1 -> x0, blocking collectives: 31.6 us -> none  [sent_together(): lax.all_to_all(both, axis, split_axis=split_dim, concat_axis=concat_dim,...]
    dot_general x2 -> x0, matrix products: 25.9 us -> none  [the longest x1 25.8 us: slot_correlation(): jnp.einsum('isn,ksn->sik', flattened, flattened, preferred_element_type=j...]
    reshape x1 -> x0, local copies, waits for them, and re-layouts: 19.3 us -> none  [slot_correlation(): residual_set.reshape(residual_set.shape[0], residual_set.shape[1], -1)]
    convert_element_type x4 -> x0, other arithmetic: 15.1 us -> none  [the longest x1 15 us: blend_history(): return running.astype(jnp.bfloat16)]
    slice x14 -> x0, local copies, waits for them, and re-layouts: 8.38 us -> none  [the longest x6 3.45 us: small_solve(): column = system[:, step_index] / system[step_index, step_index]]
    select_n x12 -> x0, other arithmetic: 6.39 us -> none  [the longest x5 4.13 us: small_solve(): column = jnp.where(positions > step_index, column, 0.0)]
where the time goes in v1:
time: 54.6 us; the launch traced here: 53.6 us
  Pallas kernels  50.1 us (92%)
  local copies, waits for them, and re-layouts  2.81 us (5%)
  between operations  0.65 us (1%)
    pallas_call x1, Pallas kernels, on_device(): pl.pallas_call(functools.partial(kernel, n_rows, n_cols), out_shape=(jax....  50.1 us
    unnamed x5, local copies, waits for them, and re-layouts  2.3 us

profile of v1, /device:TPU:1, one launch (start us, length us, event | category | flops | bytes accessed | tf_op | source)
XLA Modules:
  0.0 53.6 jit_solution(8422842292596964348)
XLA Ops:
  0.6 0.0 copy-start
  0.6 0.6 %copy-done = s32[64]{0:T(128)S(1)} copy-done((s32[64]{0:T(128)S(1)}, s32[64]{0:T(128)}, u32[]{:S(2)}) %copy-start) | copy-done | bytes 280
  1.3 0.0 copy-start.1
  1.3 0.7 %copy-done.1 = s32[2,64]{1,0:T(2,128)S(1)} copy-done((s32[2,64]{1,0:T(2,128)S(1)}, s32[2,64]{1,0:T(2,128)}, u32[]{:S(2)}) %copy-start.1) | copy-done | bytes 536
  2.0 50.1 %shard_map.59 = (bf16[32,128,128]{2,1,0:T(8,128)(2,1)S(1)}, f32[8,128]{1,0:T(8,128)S(1)}) custom-call(bf16[6,64,128,128]{3,2,1,0:T(8,128)(2,1)} %dens_hbm.1, bf16[6,64,128,128]{3,2,1,0:T(8,128)(2,1)} %res_hbm.1, s32[2,64]{1,0:T(2,128)S(1)} %copy-done.1, s32[64]{0:T(128)S(1)} %copy-done, s32[1,64]{1,0:T(1,128)S(1)} %bitcast.3), custom_call_target="tpu_custom_call" | custom-call | tf_op jit(solution)/shard_map/pallas_call | solution.py:290
  52.1 0.5 slice_bitcast_fusion
  52.6 1.0 %copy.7 = bf16[32,128,128]{2,1,0:T(8,128)(2,1)} copy(bf16[32,128,128]{2,1,0:T(8,128)(2,1)S(1)} %get-tuple-element.8) | data formatting | bytes 2097152
Async XLA Ops:
  0.6 0.7 %copy-start = (s32[64]{0:T(128)S(1)}, s32[64]{0:T(128)}, u32[]{:S(2)}) copy-start(s32[64]{0:T(128)} %owner.1) | copy-start | bytes 772
  1.3 0.7 %copy-start.1 = (s32[2,64]{1,0:T(2,128)S(1)}, s32[2,64]{1,0:T(2,128)}, u32[]{:S(2)}) copy-start(s32[2,64]{1,0:T(2,128)} %pairs.1) | copy-start | bytes 1540

commit v2 on v1

--- a/solution.py
+++ b/solution.py
@@ -14,10 +14,11 @@
 OWNED = 32
 BLOCK = 128
 CAP = 4
-CHUNK = 4
+CHUNK = 8
 N_CHUNKS = HELD // CHUNK
 GROUP = 32
 STACK = HIST * GROUP
+SEND_ORDER = [10, 6, 14, 9, 11, 2, 5, 15, 7, 13, 8, 1, 3, 4, 12]
 
 mix_weight = 0.3
 
@@ -27,11 +28,13 @@
     n_cols,
     dens_hbm,
     res_hbm,
+    pairs_hbm,
+    owner_hbm,
+    owned,
+    coef_out,
     pairs,
     owner,
     owner_row,
-    owned,
-    coef_out,
     dens,
     res,
     acc,
@@ -66,6 +69,13 @@
         part = pl.ds(c * CHUNK, CHUNK)
         return pltpu.make_async_copy(src.at[:, part], dst.at[:, part], sem.at[c])
 
+    small = [
+        pltpu.make_async_copy(owner_hbm, owner_row, table_sem.at[2]),
+        pltpu.make_async_copy(owner_hbm, owner, table_sem.at[3]),
+        pltpu.make_async_copy(pairs_hbm, pairs, table_sem.at[4]),
+    ]
+    for copy in small:
+        copy.start()
     for c in range(N_CHUNKS):
         chunk_copy(res_hbm, res, res_sem, c).start()
 
@@ -78,24 +88,17 @@
     for c in col_peers:
         pl.semaphore_signal(barrier, inc=1, device_id={"cols": c}, device_id_type=MESH)
 
-    own = jnp.broadcast_to(owner_row[...], (HELD, HELD))
-    down = lax.broadcasted_iota(jnp.int32, (HELD, HELD), 0)
-    across = lax.broadcasted_iota(jnp.int32, (HELD, HELD), 1)
-    own_down = jnp.sum(jnp.where(down == across, own, 0), axis=1, keepdims=True)
-    same_before = (own == own_down) & (across < down)
-    rank_down = jnp.sum(jnp.where(same_before, 1, 0), axis=1, keepdims=True)
-    place_down = jnp.where(own_down >= 0, own_down * CAP + rank_down, -1)
-    table_v[...] = jnp.sum(jnp.where(place_down == across, down, 0), axis=0, keepdims=True)
-    lanes = lax.broadcasted_iota(jnp.int32, (HELD, BLOCK), 1)
-    counts_out[...] = jnp.sum(jnp.where(own_down == lanes, 1, 0), axis=0, keepdims=True)
-    table_copy = pltpu.make_async_copy(table_v, table_s, table_sem.at[0])
-    table_copy.start()
+    for copy in small:
+        copy.wait()
 
     acc[...] = jnp.zeros_like(acc)
 
+    def weight_of(s):
+        live = owner[0, s] >= 0
+        return jnp.where(live, jnp.where(pairs[0, s] == pairs[1, s], 1.0, 2.0), 0.0)
+
     def gram_slot(s):
-        live = owner[s] >= 0
-        weight = jnp.where(live, jnp.where(pairs[0, s] == pairs[1, s], 1.0, 2.0), 0.0)
+        weight = weight_of(s)
         parts = [
             res[:, s, pl.ds(g * GROUP, GROUP), :].reshape(STACK, BLOCK)
             for g in range(BLOCK // GROUP)
@@ -106,13 +109,12 @@
     def gram_chunk(c, carry):
         chunk_copy(res_hbm, res, res_sem, c).wait()
         chunk_copy(dens_hbm, dens, dens_sem, c).start()
-        for h in range(CHUNK // 2):
-            pieces = [gram_slot(c * CHUNK + h * 2 + j) for j in range(2)]
-            left = jnp.concatenate([p[0] for p in pieces], axis=1)
-            right = jnp.concatenate([p[1] for p in pieces], axis=1)
-            acc[...] += lax.dot_general(
-                left, right, (((1,), (1,)), ((), ())), preferred_element_type=jnp.float32
-            )
+        pieces = [gram_slot(c * CHUNK + j) for j in range(CHUNK)]
+        left = jnp.concatenate([p[0] for p in pieces], axis=1)
+        right = jnp.concatenate([p[1] for p in pieces], axis=1)
+        acc[...] += lax.dot_general(
+            left, right, (((1,), (1,)), ((), ())), preferred_element_type=jnp.float32
+        )
         return carry
 
     lax.fori_loop(0, N_CHUNKS, gram_chunk, 0)
@@ -178,6 +180,19 @@
 
     for c in col_peers:
         cols_copy(c, my_col).start()
+    own = jnp.broadcast_to(owner_row[...], (HELD, HELD))
+    down = lax.broadcasted_iota(jnp.int32, (HELD, HELD), 0)
+    across = lax.broadcasted_iota(jnp.int32, (HELD, HELD), 1)
+    own_down = jnp.sum(jnp.where(down == across, own, 0), axis=1, keepdims=True)
+    same_before = (own == own_down) & (across < down)
+    rank_down = jnp.sum(jnp.where(same_before, 1, 0), axis=1, keepdims=True)
+    place_down = jnp.where(own_down >= 0, own_down * CAP + rank_down, -1)
+    table_v[...] = jnp.sum(jnp.where(place_down == across, down, 0), axis=0, keepdims=True)
+    lanes = lax.broadcasted_iota(jnp.int32, (HELD, BLOCK), 1)
+    counts_out[...] = jnp.sum(jnp.where(own_down == lanes, 1, 0), axis=0, keepdims=True)
+    table_copy = pltpu.make_async_copy(table_v, table_s, table_sem.at[0])
+    table_copy.start()
+
     counts_in[my_row] = counts_out[...]
     for r in row_peers:
         counts_copy(r, my_row).start()
@@ -218,7 +233,7 @@
     shown = jnp.zeros((8, BLOCK), jnp.float32)
     for i in range(HIST):
         shown = jnp.where(lane == i, coef[i], shown)
-    coef_out[...] = shown
+    coef_out[...] = shown[0:1, 0:HIST]
 
     coef_d = [c[0:1, :] for c in coef]
     coef_r = [c[0:1, :] * mix_weight for c in coef]
@@ -233,13 +248,16 @@
         return running.astype(jnp.bfloat16)
 
     def send_step(o, carry):
-        q = lax.rem(my_row + o, n_rows)
+        code = SEND_ORDER[-1]
+        for t, value in enumerate(SEND_ORDER[:-1]):
+            code = jnp.where(o == t, value, code)
+        q = lax.rem(my_row // 4 + code // 4, 4) * 4 + lax.rem(my_row + code, 4)
         for k in range(CAP):
             outgoing[q, k] = blend(q, k)
         move_copy(q, my_row).start()
         return carry
 
-    lax.fori_loop(1, n_rows, send_step, 0)
+    lax.fori_loop(0, len(SEND_ORDER), send_step, 0)
     for k in range(CAP):
         arrived[my_row * CAP + k] = blend(my_row, k)
 
@@ -268,10 +286,11 @@
         move_copy(r, r).wait_recv()
 
     def keep(p, carry):
-        owned[p] = arrived[order_s[0, p]]
+        for j in range(8):
+            owned[p * 8 + j] = arrived[order_s[0, p * 8 + j]]
         return carry
 
-    lax.fori_loop(0, OWNED, keep, 0)
+    lax.fori_loop(0, OWNED // 8, keep, 0)
 
     for c in col_peers:
         cols_copy(c, my_col).wait_send()
@@ -279,6 +298,17 @@
         counts_copy(r, my_row).wait_send()
         rows_copy(r, my_row).wait_send()
         move_copy(r, my_row).wait_send()
+
+
+def put_out(owned, coef, owned_out, coef_out, sem):
+    copies = [
+        pltpu.make_async_copy(owned, owned_out, sem.at[0]),
+        pltpu.make_async_copy(coef, coef_out, sem.at[1]),
+    ]
+    for copy in copies:
+        copy.start()
+    for copy in copies:
+        copy.wait()
 
 
 def solution(mesh):
@@ -291,20 +321,22 @@
             functools.partial(kernel, n_rows, n_cols),
             out_shape=(
                 jax.ShapeDtypeStruct((OWNED, BLOCK, BLOCK), jnp.bfloat16),
-                jax.ShapeDtypeStruct((8, BLOCK), jnp.float32),
+                jax.ShapeDtypeStruct((1, HIST), jnp.float32),
             ),
             in_specs=[
                 pl.BlockSpec(memory_space=pl.ANY),
                 pl.BlockSpec(memory_space=pl.ANY),
-                pl.BlockSpec(memory_space=pltpu.SMEM),
-                pl.BlockSpec(memory_space=pltpu.SMEM),
-                pl.BlockSpec(memory_space=pltpu.VMEM),
+                pl.BlockSpec(memory_space=pltpu.HBM),
+                pl.BlockSpec(memory_space=pltpu.HBM),
             ],
             out_specs=(
                 pl.BlockSpec(memory_space=pltpu.VMEM),
                 pl.BlockSpec(memory_space=pltpu.VMEM),
             ),
             scratch_shapes=[
+                pltpu.SMEM((2, HELD), jnp.int32),
+                pltpu.SMEM((1, HELD), jnp.int32),
+                vmem((1, HELD), jnp.int32),
                 vmem((HIST, HELD, BLOCK, BLOCK), jnp.bfloat16),
                 vmem((HIST, HELD, BLOCK, BLOCK), jnp.bfloat16),
                 vmem((STACK, STACK), jnp.float32),
@@ -330,13 +362,29 @@
                 dma((n_rows,)),
                 dma((n_rows,)),
                 dma((n_rows,)),
-                dma((2,)),
+                dma((5,)),
             ],
             compiler_params=pltpu.CompilerParams(
                 collective_id=0, has_side_effects=True, vmem_limit_bytes=48 * 1024 * 1024
             ),
-        )(densities, residuals, block_pairs, new_owner, new_owner.reshape(1, HELD))
-        return owned, coef[0, :HIST]
+        )(
+            densities,
+            residuals,
+            pltpu.with_memory_space_constraint(block_pairs, pltpu.HBM),
+            pltpu.with_memory_space_constraint(new_owner.reshape(1, HELD), pltpu.HBM),
+        )
+        owned, coef = pl.pallas_call(
+            put_out,
+            out_shape=(
+                jax.ShapeDtypeStruct((OWNED, BLOCK, BLOCK), jnp.bfloat16),
+                jax.ShapeDtypeStruct((1, HIST), jnp.float32),
+            ),
+            in_specs=[pl.BlockSpec(memory_space=pltpu.VMEM)] * 2,
+            out_specs=(pl.BlockSpec(memory_space=pltpu.HBM),) * 2,
+            scratch_shapes=[dma((2,))],
+            compiler_params=pltpu.CompilerParams(vmem_limit_bytes=2 * 1024 * 1024),
+        )(owned, coef)
+        return owned, coef.reshape(HIST)
 
     placed = P(None, ("rows", "cols"), None, None)
     return jax.shard_map(

time: 54.6 us -> 49.9 us (0.914); the launches traced: 53.6 us -> 49.8 us
  local copies, waits for them, and re-layouts: 2.81 us -> 0 us
  Pallas kernels: 50.1 us -> 49.1 us
    unnamed x5 -> x0, local copies, waits for them, and re-layouts: 2.3 us -> none
    pallas_call x1, Pallas kernels: 50.1 us -> 48.1 us  [on_device(): pl.pallas_call(functools.partial(kernel, n_rows, n_cols), out_shape=(jax....]
    pallas_call x0 -> x1, Pallas kernels: none -> 0.99 us  [on_device(): pl.pallas_call(put_out, out_shape=(jax.ShapeDtypeStruct((OWNED, BLOCK, BL...]
where the time goes in v2:
time: 49.9 us; the launch traced here: 49.8 us
  Pallas kernels  49.1 us (98%)
  between operations  0.64 us (1%)
    pallas_call x1, Pallas kernels, on_device(): pl.pallas_call(functools.partial(kernel, n_rows, n_cols), out_shape=(jax....  48.1 us

profile of v2, /device:TPU:1, one launch (start us, length us, event | category | flops | bytes accessed | tf_op | source)
XLA Modules:
  0.0 49.8 jit_solution(14999525920136545648)
XLA Ops:
  0.6 48.1 %shard_map.59 = (bf16[32,128,128]{2,1,0:T(8,128)(2,1)S(1)}, f32[1,6]{1,0:T(1,128)S(1)}) custom-call(bf16[6,64,128,128]{3,2,1,0:T(8,128)(2,1)} %dens_hbm.1, bf16[6,64,128,128]{3,2,1,0:T(8,128)(2,1)} %res_hbm.1, s32[2,64]{1,0:T(2,128)} %pairs_hbm.1, s32[1,64]{1,0:T(1,128)} %bitcast.2), custom_call_target="tpu_custom_call" | custom-call | tf_op jit(solution)/shard_map/pallas_call | solution.py:320
  48.8 1.0 %shard_map.60 = (bf16[32,128,128]{2,1,0:T(8,128)(2,1)}, f32[1,6]{1,0:T(1,128)}) custom-call(bf16[32,128,128]{2,1,0:T(8,128)(2,1)S(1)} %get-tuple-element.6.owned, f32[1,6]{1,0:T(1,128)S(1)} %get-tuple-element.7.coef), custom_call_target="tpu_custom_call" | custom-call | tf_op jit(solution)/shard_map/pallas_call | solution.py:376

commit v3 on v2

--- a/solution.py
+++ b/solution.py
@@ -14,11 +14,13 @@
 OWNED = 32
 BLOCK = 128
 CAP = 4
-CHUNK = 8
+CHUNK = 16
 N_CHUNKS = HELD // CHUNK
-GROUP = 32
+GROUP = 16
 STACK = HIST * GROUP
 SEND_ORDER = [10, 6, 14, 9, 11, 2, 5, 15, 7, 13, 8, 1, 3, 4, 12]
+
+COL_ORDER = [4, 3, 5, 2, 6, 1, 7]
 
 mix_weight = 0.3
 
@@ -79,8 +81,10 @@
     for c in range(N_CHUNKS):
         chunk_copy(res_hbm, res, res_sem, c).start()
 
-    row_peers = [lax.rem(my_row + o, n_rows) for o in range(1, n_rows)]
-    col_peers = [lax.rem(my_col + o, n_cols) for o in range(1, n_cols)]
+    row_peers = [
+        lax.rem(my_row // 4 + code // 4, 4) * 4 + lax.rem(my_row + code, 4) for code in SEND_ORDER
+    ]
+    col_peers = [lax.rem(my_col + o, n_cols) for o in COL_ORDER]
 
     barrier = pltpu.get_barrier_semaphore()
     for r in row_peers:
@@ -109,12 +113,13 @@
     def gram_chunk(c, carry):
         chunk_copy(res_hbm, res, res_sem, c).wait()
         chunk_copy(dens_hbm, dens, dens_sem, c).start()
-        pieces = [gram_slot(c * CHUNK + j) for j in range(CHUNK)]
-        left = jnp.concatenate([p[0] for p in pieces], axis=1)
-        right = jnp.concatenate([p[1] for p in pieces], axis=1)
-        acc[...] += lax.dot_general(
-            left, right, (((1,), (1,)), ((), ())), preferred_element_type=jnp.float32
-        )
+        for h in range(2):
+            pieces = [gram_slot(c * CHUNK + h * (CHUNK // 2) + j) for j in range(CHUNK // 2)]
+            left = jnp.concatenate([p[0] for p in pieces], axis=1)
+            right = jnp.concatenate([p[1] for p in pieces], axis=1)
+            acc[h] += lax.dot_general(
+                left, right, (((1,), (1,)), ((), ())), preferred_element_type=jnp.float32
+            )
         return carry
 
     lax.fori_loop(0, N_CHUNKS, gram_chunk, 0)
@@ -122,7 +127,7 @@
     x_down = lax.broadcasted_iota(jnp.int32, (STACK, STACK), 0)
     x_across = lax.broadcasted_iota(jnp.int32, (STACK, STACK), 1)
     same_x = lax.rem(x_down, GROUP) == lax.rem(x_across, GROUP)
-    diag = jnp.where(same_x, acc[...], 0.0).reshape(HIST, GROUP, STACK)
+    diag = jnp.where(same_x, jnp.sum(acc[...], axis=0), 0.0).reshape(HIST, GROUP, STACK)
     by_iterate = jnp.sum(diag, axis=1)
     seg = lax.broadcasted_iota(jnp.int32, (HIST, STACK), 1) // GROUP
     i_at = lax.broadcasted_iota(jnp.int32, (HIST, BLOCK), 0)
@@ -339,7 +344,7 @@
                 vmem((1, HELD), jnp.int32),
                 vmem((HIST, HELD, BLOCK, BLOCK), jnp.bfloat16),
                 vmem((HIST, HELD, BLOCK, BLOCK), jnp.bfloat16),
-                vmem((STACK, STACK), jnp.float32),
+                vmem((2, STACK, STACK), jnp.float32),
                 vmem((n_rows, CAP, BLOCK, BLOCK), jnp.bfloat16),
                 vmem((n_rows * CAP, BLOCK, BLOCK), jnp.bfloat16),
                 vmem((n_cols, 1, BLOCK), jnp.float32),

time: 49.9 us -> 47.7 us (0.956)
  Pallas kernels: 49.1 us -> 47 us
    pallas_call x1, Pallas kernels: 48.1 us -> 46 us  [on_device(): pl.pallas_call(functools.partial(kernel, n_rows, n_cols), out_shape=(jax....]
where the time goes in v3:
time: 47.7 us; the launch traced here: 47.6 us
  Pallas kernels  47 us (99%)
  between operations  0.64 us (1%)
    pallas_call x1, Pallas kernels, on_device(): pl.pallas_call(functools.partial(kernel, n_rows, n_cols), out_shape=(jax....  46 us
    pallas_call x1, Pallas kernels, on_device(): pl.pallas_call(put_out, out_shape=(jax.ShapeDtypeStruct((OWNED, BLOCK, BL...  0.99 us

profile of v3, /device:TPU:1, one launch (start us, length us, event | category | flops | bytes accessed | tf_op | source)
XLA Modules:
  0.0 47.6 jit_solution(3691960847635502769)
XLA Ops:
  0.6 46.0 %shard_map.59 = (bf16[32,128,128]{2,1,0:T(8,128)(2,1)S(1)}, f32[1,6]{1,0:T(1,128)S(1)}) custom-call(bf16[6,64,128,128]{3,2,1,0:T(8,128)(2,1)} %dens_hbm.1, bf16[6,64,128,128]{3,2,1,0:T(8,128)(2,1)} %res_hbm.1, s32[2,64]{1,0:T(2,128)} %pairs_hbm.1, s32[1,64]{1,0:T(1,128)} %bitcast.2), custom_call_target="tpu_custom_call" | custom-call | tf_op jit(solution)/shard_map/pallas_call | solution.py:325
  46.6 1.0 %shard_map.60 = (bf16[32,128,128]{2,1,0:T(8,128)(2,1)}, f32[1,6]{1,0:T(1,128)}) custom-call(bf16[32,128,128]{2,1,0:T(8,128)(2,1)S(1)} %get-tuple-element.6.owned, f32[1,6]{1,0:T(1,128)S(1)} %get-tuple-element.7.coef), custom_call_target="tpu_custom_call" | custom-call | tf_op jit(solution)/shard_map/pallas_call | solution.py:381

commit v4 on v3

--- a/solution.py
+++ b/solution.py
@@ -113,8 +113,8 @@
     def gram_chunk(c, carry):
         chunk_copy(res_hbm, res, res_sem, c).wait()
         chunk_copy(dens_hbm, dens, dens_sem, c).start()
-        for h in range(2):
-            pieces = [gram_slot(c * CHUNK + h * (CHUNK // 2) + j) for j in range(CHUNK // 2)]
+        for h in range(1):
+            pieces = [gram_slot(c * CHUNK + h * (CHUNK // 1) + j) for j in range(CHUNK // 1)]
             left = jnp.concatenate([p[0] for p in pieces], axis=1)
             right = jnp.concatenate([p[1] for p in pieces], axis=1)
             acc[h] += lax.dot_general(
@@ -344,7 +344,7 @@
                 vmem((1, HELD), jnp.int32),
                 vmem((HIST, HELD, BLOCK, BLOCK), jnp.bfloat16),
                 vmem((HIST, HELD, BLOCK, BLOCK), jnp.bfloat16),
-                vmem((2, STACK, STACK), jnp.float32),
+                vmem((1, STACK, STACK), jnp.float32),
                 vmem((n_rows, CAP, BLOCK, BLOCK), jnp.bfloat16),
                 vmem((n_rows * CAP, BLOCK, BLOCK), jnp.bfloat16),
                 vmem((n_cols, 1, BLOCK), jnp.float32),

time: 47.7 us -> 47.7 us (level)
  no operation moved by 1% of the time
where the time goes in v4:
time: 47.7 us; the launch traced here: 47.6 us
  Pallas kernels  47 us (99%)
  between operations  0.64 us (1%)
    pallas_call x1, Pallas kernels, on_device(): pl.pallas_call(functools.partial(kernel, n_rows, n_cols), out_shape=(jax....  46 us
    pallas_call x1, Pallas kernels, on_device(): pl.pallas_call(put_out, out_shape=(jax.ShapeDtypeStruct((OWNED, BLOCK, BL...  0.99 us

profile of v4, /device:TPU:1, one launch (start us, length us, event | category | flops | bytes accessed | tf_op | source)
XLA Modules:
  0.0 47.6 jit_solution(13050537364830466535)
XLA Ops:
  0.6 46.0 %shard_map.59 = (bf16[32,128,128]{2,1,0:T(8,128)(2,1)S(1)}, f32[1,6]{1,0:T(1,128)S(1)}) custom-call(bf16[6,64,128,128]{3,2,1,0:T(8,128)(2,1)} %dens_hbm.1, bf16[6,64,128,128]{3,2,1,0:T(8,128)(2,1)} %res_hbm.1, s32[2,64]{1,0:T(2,128)} %pairs_hbm.1, s32[1,64]{1,0:T(1,128)} %bitcast.2), custom_call_target="tpu_custom_call" | custom-call | tf_op jit(solution)/shard_map/pallas_call | solution.py:325
  46.6 1.0 %shard_map.60 = (bf16[32,128,128]{2,1,0:T(8,128)(2,1)}, f32[1,6]{1,0:T(1,128)}) custom-call(bf16[32,128,128]{2,1,0:T(8,128)(2,1)S(1)} %get-tuple-element.6.owned, f32[1,6]{1,0:T(1,128)S(1)} %get-tuple-element.7.coef), custom_call_target="tpu_custom_call" | custom-call | tf_op jit(solution)/shard_map/pallas_call | solution.py:381
